TPU v7x, 32 devices: a whole 2x2x4 slice. The times are simulated.
32 devices in a mesh: seq: 8 (over y, x, core), mp: 4 (over z).
Axes of the slice: x: 2, y: 2, z: 4, core: 2. Of those that a mesh axis runs over, the one named last changes fastest.
Arguments:
- inputs: bfloat16 [8192, 4096], P('seq', 'mp'), may hold values from -6 to 6
- conv_weight: bfloat16 [4, 4096], P(None, 'mp'), may hold values from -3 to 3
- conv_bias: bfloat16 [4096], P('mp'), may hold values from -3 to 3
- doc_start: int32 [8192], P('seq'), may hold values from 0 to 8191, as said below
- counts: int32 [8], P('seq'), may hold values from 341 to 1024
Outputs:
- gram: float32 [4096, 4096], P('seq', 'mp')
Inputs may be any that keep to these rules, and one draw needn't show every extreme that they name: doc_start is never above the token's own position, and for t > 0 either doc_start[t] == t or doc_start[t] == doc_start[t - 1]; doc_start[0] is 0.
All inputs are finite; a program needn't handle non-finite values.
Results may differ from a plain program's by a relative error of at most 0.0003.
Values may be sent and summed in bfloat16 or wider, within the bound.
A program may use at most 64 MiB of HBM per device.

v0:
```python
import jax
import jax.numpy as jnp
from jax import lax
from jax.sharding import PartitionSpec as P


def passed_along(x, axis, by):
    peers = lax.axis_size(axis)
    pairs = [(i, i + by) for i in range(peers) if 0 <= i + by < peers]
    return lax.ppermute(x, axis, pairs)


def causal_conv(extended, weights, bias, position, doc_start, length):
    kernel_len = weights.shape[0]
    summed = jnp.zeros((length, weights.shape[1]), jnp.float32) + bias.astype(jnp.float32)
    for lag in range(kernel_len):
        window = extended[kernel_len - 1 - lag : kernel_len - 1 - lag + length].astype(jnp.float32)
        usable = position - lag >= doc_start
        summed = summed + jnp.where(usable[:, None], weights[lag].astype(jnp.float32) * window, 0.0)
    return jax.nn.silu(summed).astype(jnp.bfloat16)


def on_device(inputs, conv_weight, conv_bias, doc_start, counts):
    row_count = inputs.shape[0]
    kernel_len = conv_weight.shape[0]
    position = lax.axis_index("seq") * row_count + jnp.arange(row_count, dtype=jnp.int32)
    counted = jnp.arange(row_count, dtype=jnp.int32) < counts[0]
    token_total = lax.psum(counts.astype(jnp.float32)[0], "seq")
    prior = passed_along(inputs[row_count - (kernel_len - 1) :], "seq", 1)
    extended = jnp.concatenate([prior, inputs], axis=0)
    own_feats = causal_conv(extended, conv_weight, conv_bias, position, doc_start, row_count)
    kept = jnp.where(counted[:, None], own_feats, jnp.zeros_like(own_feats))
    whole = lax.all_gather(own_feats, "mp", axis=1, tiled=True)
    summed = lax.psum_scatter(
        lax.dot_general(whole, kept, (((0,), (0,)), ((), ())), preferred_element_type=jnp.float32),
        "seq",
        scatter_dimension=0,
        tiled=True,
    )
    return summed / token_total


def solution(mesh):
    placed = (P("seq", "mp"), P(None, "mp"), P("mp"), P("seq"), P("seq"))
    return jax.shard_map(
        on_device, mesh=mesh, in_specs=placed, out_specs=P("seq", "mp"), check_vma=False
    )
```

profile of v0, /device:TPU:0, one launch (start us, length us, event | category | flops | bytes accessed | tf_op | source)
XLA Modules:
  0.0 316.0 jit_solution(3767885994745322081)
XLA Ops:
  6.5 0.0 all-gather.2.cloned.1.call-start
  6.5 0.7 slice.26
  7.3 2.4 collective-permute-start
  9.7 0.9 slice_convert_fusion.3
  10.5 0.7 fusion.6
  11.2 0.7 convert_element_type.29
  11.9 0.0 collective-permute-done
  11.9 9.8 %multiply_convert_fusion = bf16[1024,1024]{1,0:T(8,128)(2,1)} fusion(bf16[1024,1024]{1,0:T(8,128)(2,1)} %param.5, bf16[3,1024]{1,0:T(4,128)(2,1)S(1)} %collective-permute-done, f32[1024]{0:T(1024)S(1)} %bitcast.10, f32[1024]{0:T(1024)S(1)} %bitcast.11, f32[1024]{0:T(1024)S(1)} %bitcast.9, f32[1024]{0:T(1024)S(1)} %bitcast.8, f32[1024]{0:T(1024)S(1)} %convert_element_type.29, ...), kind=kLoop, calls=%fused_computation | loop fusion | flops 31457280 | bytes 4225024 | tf_op jit(solution)/shard_map/convert_element_type | solution.py:20
  21.7 0.0 all-gather.2.cloned.1.call-update
  21.7 0.0 reduce-scatter.2.cloned.1.call-start
  22.4 152.1 %all-gather.2.cloned.1.call-done = bf16[1024,4096]{1,0:T(8,128)(2,1)} async-done(((bf16[1024,1024]{1,0:T(8,128)(2,1)}), bf16[1024,4096]{1,0:T(8,128)(2,1)}) %all-gather.2.cloned.1.call-update) | async-done | bytes 8388624 | tf_op jit(solution)/shard_map/all_gather | solution.py:33
  174.5 16.3 %fusion.2 = f32[4096,1024]{1,0:T(8,128)} fusion(bf16[1024,4096]{1,0:T(8,128)(2,1)} %all-gather.2.cloned.1.call-done, bf16[1024,1024]{1,0:T(8,128)(2,1)} %multiply_convert_fusion, pred[1024]{0:T(1024)(128)(4,1)S(1)} %iota_compare_fusion), kind=kOutput, calls=%fused_computation.6 | convolution fusion | flops 8590983168 | bytes 27264000 | tf_op jit(solution)/shard_map/dot_general | solution.py:35
  190.8 0.0 reduce-scatter.2.cloned.1.call-update
  190.9 15.0 %psum.7 = f32[]{:T(128)} all-reduce(f32[]{:T(128)} %bitcast.5), channel_id=1, replica_groups=mesh['seq'=8,'mp'=4] {'seq'}, use_global_device_ids=true, to_apply=%region_1.2 | all-reduce | flops 1 | bytes 8 | tf_op jit(solution)/shard_map/psum | solution.py:28
  205.8 99.5 %reduce-scatter.2.cloned.1.call-done = f32[512,1024]{1,0:T(8,128)} async-done(((f32[4096,1024]{1,0:T(8,128)}), f32[512,1024]{1,0:T(8,128)}) %reduce-scatter.2.cloned.1.call-update) | async-done | bytes 2097168 | tf_op jit(solution)/shard_map/reduce_scatter | solution.py:34
  305.4 3.8 %broadcast_divide_fusion = f32[512,1024]{1,0:T(8,128)} fusion(f32[512,1024]{1,0:T(8,128)} %reduce-scatter.2.cloned.1.call-done, f32[]{:T(128)} %psum.7), kind=kLoop, calls=%fused_computation.9 | loop fusion | flops 524288 | bytes 4194308 | tf_op jit(solution)/shard_map/div | solution.py:40
  (1 shorter events, 0.0 us)
Async XLA Ops:
  6.5 168.0 %all-gather.2.cloned.1.call-start = ((), (), s32[]{:S(2)}) async-start(), calls=%async_computation.1 | async-start | bytes 10485760 | tf_op jit(solution)/shard_map/all_gather | solution.py:33
  7.3 4.7 %collective-permute-start = (bf16[3,1024]{1,0:T(4,128)(2,1)S(1)}, bf16[3,1024]{1,0:T(4,128)(2,1)S(1)}, u32[]{:S(2)}, u32[]{:S(2)}) collective-permute-start(bf16[3,1024]{1,0:T(4,128)(2,1)S(1)} %slice.26), channel_id=1, source_target_pairs={{0,4},{4,8},{8,12},{12,16},{16,20},{20,24},{24,28},{1,5},{5,9},{9,... | collective-permute-start | bytes 18440 | tf_op jit(solution)/shard_map/ppermute | solution.py:10
  21.7 283.7 %reduce-scatter.2.cloned.1.call-start = ((), (), s32[]{:S(2)}) async-start(), calls=%async_computation.2 | async-start | bytes 18874368 | tf_op jit(solution)/shard_map/reduce_scatter | solution.py:34
Sparse Core Ops, SparseCore 0:
  21.8 152.6 all-gather.1
  191.0 114.3 reduce-scatter.1
where the time goes:
time: 316 us
  waiting for transfers between devices  252 us (80%)
  matrix products  16.3 us (5%)
  other arithmetic  15.9 us (5%)
  blocking collectives  15 us (5%)
  between operations  14.1 us (4%)
    all_gather x1, waiting for transfers between devices, on_device(): whole = lax.all_gather(own_feats, 'mp', axis=1, tiled=True)  152 us
    reduce_scatter x1, waiting for transfers between devices, on_device(): lax.psum_scatter(lax.dot_general(whole, kept, (((0,), (0,)), ((), ())), p...  99.5 us
    dot_general x1, matrix products, on_device(): lax.dot_general(whole, kept, (((0,), (0,)), ((), ())), preferred_element_...  16.3 us
    psum x1, blocking collectives, on_device(): token_total = lax.psum(counts.astype(jnp.float32)[0], 'seq')  15 us
    convert_element_type x1, other arithmetic, causal_conv(): return jax.nn.silu(summed).astype(jnp.bfloat16)  9.78 us
  transfers between devices with their start and end apart: 3, of which 2 were waited for; matrix products, arithmetic and copies ran while one was open for 1% of the time, Pallas kernels for 0%

commit v1 on v0

--- a/solution.py
+++ b/solution.py
@@ -30,7 +30,10 @@
     extended = jnp.concatenate([prior, inputs], axis=0)
     own_feats = causal_conv(extended, conv_weight, conv_bias, position, doc_start, row_count)
     kept = jnp.where(counted[:, None], own_feats, jnp.zeros_like(own_feats))
-    whole = lax.all_gather(own_feats, "mp", axis=1, tiled=True)
+    all_rows = []
+    for _ in range(jax.lax.axis_size("mp")):
+        all_rows.append(own_feats)
+    whole = jnp.concatenate(jax.lax.all_to_all(jnp.stack(all_rows, axis=0), "mp", 0, 0), axis=1)
     summed = lax.psum_scatter(
         lax.dot_general(whole, kept, (((0,), (0,)), ((), ())), preferred_element_type=jnp.float32),
         "seq",

time: 316 us -> 361 us (1.14)
  waiting for transfers between devices: 252 us -> 286 us
  local copies, waits for them, and re-layouts: 0.72 us -> 7.9 us
  starting transfers between devices: 2.43 us -> 8.21 us
    all_to_all x0 -> x1, waiting for transfers between devices: none -> 183 us  [on_device(): jax.lax.all_to_all(jnp.stack(all_rows, axis=0), 'mp', 0, 0)]
    all_gather x1 -> x0, waiting for transfers between devices: 152 us -> none  [on_device(): whole = lax.all_gather(own_feats, 'mp', axis=1, tiled=True)]
    all_to_all x0 -> x1, starting transfers between devices: none -> 5.82 us  [on_device(): jax.lax.all_to_all(jnp.stack(all_rows, axis=0), 'mp', 0, 0)]
    another operation x0 -> x1, local copies, waits for them, and re-layouts: none -> 4.32 us  [on_device(): jnp.stack(all_rows, axis=0)]
where the time goes in v1:
time: 361 us
  waiting for transfers between devices  286 us (79%)
  other arithmetic  15.9 us (4%)
  matrix products  14.6 us (4%)
  between operations  14.1 us (4%)
  blocking collectives  14 us (4%)
  starting transfers between devices  8.21 us (2%)
  local copies, waits for them, and re-layouts  7.9 us (2%)
    all_to_all x1, waiting for transfers between devices, on_device(): jax.lax.all_to_all(jnp.stack(all_rows, axis=0), 'mp', 0, 0)  183 us
    reduce_scatter x1, waiting for transfers between devices, on_device(): lax.psum_scatter(lax.dot_general(whole, kept, (((0,), (0,)), ((), ())), p...  103 us
    dot_general x1, matrix products, on_device(): lax.dot_general(whole, kept, (((0,), (0,)), ((), ())), preferred_element_...  14.6 us
    psum x1, blocking collectives, on_device(): token_total = lax.psum(counts.astype(jnp.float32)[0], 'seq')  14 us
    convert_element_type x1, other arithmetic, causal_conv(): return jax.nn.silu(summed).astype(jnp.bfloat16)  9.83 us
  transfers between devices with their start and end apart: 3, of which 2 were waited for; matrix products, arithmetic and copies ran while one was open for 1% of the time, Pallas kernels for 0%

profile of v1, /device:TPU:0, one launch (start us, length us, event | category | flops | bytes accessed | tf_op | source)
XLA Modules:
  0.0 360.7 jit_solution(5523192051224670768)
XLA Ops:
  6.5 0.7 slice.26
  7.3 2.4 collective-permute-start
  9.7 0.9 slice_convert_fusion.3
  10.5 0.7 fusion.6
  11.2 0.7 convert_element_type.29
  11.9 0.0 collective-permute-done
  11.9 9.8 %multiply_convert_fusion = bf16[1024,1024]{1,0:T(8,128)(2,1)} fusion(bf16[1024,1024]{1,0:T(8,128)(2,1)} %param.5, bf16[3,1024]{1,0:T(4,128)(2,1)S(1)} %collective-permute-done, f32[1024]{0:T(1024)S(1)} %bitcast.13, f32[1024]{0:T(1024)S(1)} %bitcast.14, f32[1024]{0:T(1024)S(1)} %bitcast.12, f32[1024]{0:T(1024)S(1)} %bitcast.11, ...), kind=kLoop, calls=%fused_computation | loop fusion | flops 31457280 | bytes 4225024 | tf_op jit(solution)/shard_map/convert_element_type | solution.py:20
  21.7 2.9 copy.6
  24.6 4.3 %stack.2 = bf16[4,1024,1024]{1,2,0:T(8,128)(2,1)} broadcast(bf16[1024,1024]{0,1:T(8,128)(2,1)S(1)} %copy.6), dimensions={1,2} | broadcast | bytes 10485760 | tf_op jit(solution)/shard_map/stack | solution.py:36
  28.9 0.0 copy-start
  28.9 5.8 %all-to-all-start = ((bf16[4,1024,1024]{1,2,0:T(8,128)(2,1)}), bf16[4,1024,1024]{1,2,0:T(8,128)(2,1)}, u32[]{:S(2)}, u32[]{:S(2)}) async-start(bf16[4,1024,1024]{1,2,0:T(8,128)(2,1)} %stack.2), calls=%async_computation | async-start | bytes 16777216 | tf_op jit(solution)/shard_map/all_to_all | solution.py:36
  34.7 0.0 reduce-scatter.2.cloned.1.call-start
  35.4 183.1 %all-to-all-done = bf16[4,1024,1024]{1,2,0:T(8,128)(2,1)} async-done(((bf16[4,1024,1024]{1,2,0:T(8,128)(2,1)}), bf16[4,1024,1024]{1,2,0:T(8,128)(2,1)}, u32[]{:S(2)}, u32[]{:S(2)}) %all-to-all-start) | async-done | bytes 8388640 | tf_op jit(solution)/shard_map/all_to_all | solution.py:36
  218.5 0.0 copy-done
  218.5 14.6 %fusion.2 = f32[4096,1024]{1,0:T(8,128)} fusion(bf16[1024,4096]{0,1:T(8,128)(2,1)} %bitcast.5, bf16[1024,1024]{1,0:T(8,128)(2,1)S(1)} %copy-done, pred[1024]{0:T(1024)(128)(4,1)S(1)} %iota_compare_fusion), kind=kOutput, calls=%fused_computation.6 | convolution fusion | flops 8590983168 | bytes 27264000 | tf_op jit(solution)/shard_map/dot_general | solution.py:38
  233.2 0.0 reduce-scatter.2.cloned.1.call-update
  233.2 14.0 %psum.7 = f32[]{:T(128)} all-reduce(f32[]{:T(128)} %bitcast.7), channel_id=1, replica_groups=mesh['seq'=8,'mp'=4] {'seq'}, use_global_device_ids=true, to_apply=%region_1.2 | all-reduce | flops 1 | bytes 8 | tf_op jit(solution)/shard_map/psum | solution.py:28
  247.2 102.8 %reduce-scatter.2.cloned.1.call-done = f32[512,1024]{1,0:T(8,128)} async-done(((f32[4096,1024]{1,0:T(8,128)}), f32[512,1024]{1,0:T(8,128)}) %reduce-scatter.2.cloned.1.call-update) | async-done | bytes 2097168 | tf_op jit(solution)/shard_map/reduce_scatter | solution.py:37
  350.0 3.8 %broadcast_divide_fusion = f32[512,1024]{1,0:T(8,128)} fusion(f32[512,1024]{1,0:T(8,128)} %reduce-scatter.2.cloned.1.call-done, f32[]{:T(128)} %psum.7), kind=kLoop, calls=%fused_computation.9 | loop fusion | flops 524288 | bytes 4194308 | tf_op jit(solution)/shard_map/div | solution.py:43
  (1 shorter events, 0.0 us)
Async XLA Ops:
  7.3 4.7 %collective-permute-start = (bf16[3,1024]{1,0:T(4,128)(2,1)S(1)}, bf16[3,1024]{1,0:T(4,128)(2,1)S(1)}, u32[]{:S(2)}, u32[]{:S(2)}) collective-permute-start(bf16[3,1024]{1,0:T(4,128)(2,1)S(1)} %slice.26), channel_id=1, source_target_pairs={{0,4},{4,8},{8,12},{12,16},{16,20},{20,24},{24,28},{1,5},{5,9},{9,... | collective-permute-start | bytes 18440 | tf_op jit(solution)/shard_map/ppermute | solution.py:10
  28.9 189.6 %copy-start = (bf16[1024,1024]{1,0:T(8,128)(2,1)S(1)}, bf16[1024,1024]{1,0:T(8,128)(2,1)}, u32[]{:S(2)}) copy-start(bf16[1024,1024]{1,0:T(8,128)(2,1)} %multiply_convert_fusion) | copy-start | bytes 6291460
  28.9 189.6 %all-to-all-start = ((bf16[4,1024,1024]{1,2,0:T(8,128)(2,1)}), bf16[4,1024,1024]{1,2,0:T(8,128)(2,1)}, u32[]{:S(2)}, u32[]{:S(2)}) async-start(bf16[4,1024,1024]{1,2,0:T(8,128)(2,1)} %stack.2), calls=%async_computation | async-start | bytes 16777216 | tf_op jit(solution)/shard_map/all_to_all | solution.py:36
  34.7 315.3 %reduce-scatter.2.cloned.1.call-start = ((), (), s32[]{:S(2)}) async-start(), calls=%async_computation.2 | async-start | bytes 18874368 | tf_op jit(solution)/shard_map/reduce_scatter | solution.py:37
Sparse Core Ops, SparseCore 0:
  233.3 116.6 reduce-scatter.1
